TPU v7x, 256 devices: a whole 4x4x8 slice. The times are simulated.
256 devices in a mesh: col: 128 (over x, z, y), sec: 2 (over core).
Axes of the slice: x: 4, y: 4, z: 8, core: 2. Of those that a mesh axis runs over, the one named last changes fastest.
Arguments:
- mps: bfloat16 [128, 96, 6, 6, 96], P('col', 'sec'), may hold values from -6 to 6
- ket: bfloat16 [128, 6, 6, 6, 6, 2], P('col'), may hold values from -6 to 6
- left_proj: bfloat16 [128, 96, 96, 6, 6], P('col', 'sec'), may hold values from -0.109375 to 0.109375
- right_proj: bfloat16 [128, 96, 6, 6, 96], P('col', None, None, None, 'sec'), may hold values from -0.109375 to 0.109375
- bond_charge: int32 [128, 96], P('col'), may hold values from 0 to 5
- new_charge: int32 [128, 96], P('col'), may hold values from 0 to 5
- link_charge: int32 [128, 6], P('col'), may hold values from 0 to 2
- vert_charge: int32 [128, 2, 6], P('col'), may hold values from 0 to 2
Outputs:
- new_mps: bfloat16 [128, 96, 6, 6, 96], P('col', 'sec')
- log_norm: float32 [], replicated
All inputs are finite; a program needn't handle non-finite values.
Results may differ from a plain program's by a relative error of at most 0.0064.
Values may be sent and summed in bfloat16 or wider, within the bound.
A program may use at most 192 MiB of HBM per device.

v0:
```python
import functools
import jax
import jax.numpy as jnp
from jax import lax
from jax.sharding import Mesh
from jax.sharding import PartitionSpec as P

COL = ("col_0", "col_1", "col_2")


def from_behind(x, axis, by):
    count = lax.axis_size(axis)
    return lax.ppermute(x, axis, [(i, (i + by) % count) for i in range(count)])


def joined_along(tiles, dim):
    tiles = jnp.moveaxis(tiles, 0, dim)
    shape = tiles.shape
    return tiles.reshape(*shape[:dim], shape[dim] * shape[dim + 1], *shape[dim + 2 :])


def copy_for_each(x, axis):
    count = lax.axis_size(axis)
    return lax.all_to_all(jnp.broadcast_to(x[None], (count, *x.shape)), axis, 0, 0, tiled=True)


def gather_directly(x, axis, dim):
    return joined_along(copy_for_each(x, axis), dim)


def gathered_total(x, axis):
    tiles = lax.all_gather(x, axis)
    return tiles.sum(axis=0)


def one_axis_at_a_time(x, axes):
    return functools.reduce(lax.psum, axes, x)


def absorb(
    mps_site,
    ket_site,
    left_site,
    right_site,
    charge_here,
    charge_next,
    fresh_here,
    fresh_next,
    link_here,
    link_next,
    vertical,
):
    upper = vertical[0]
    lower = vertical[1]
    physical = jnp.arange(ket_site.shape[4], dtype=jnp.int32)
    keep_mps = (
        charge_here[:, None, None, None] + upper[None, :, None, None] - upper[None, None, :, None]
        == charge_next[None, None, None, :]
    )
    masked_mps = jnp.where(keep_mps, mps_site, jnp.zeros_like(mps_site))
    keep_ket = (
        upper[:, None, None, None, None] + link_here[None, :, None, None, None]
        == lower[None, None, :, None, None]
        + link_next[None, None, None, :, None]
        + physical[None, None, None, None, :]
    )
    masked_ket = jnp.where(keep_ket, ket_site, jnp.zeros_like(ket_site))
    keep_left = (
        fresh_here[:, None, None, None]
        == charge_here[None, :, None, None]
        + link_here[None, None, :, None]
        - link_here[None, None, None, :]
    )
    masked_left = jnp.where(keep_left, left_site, jnp.zeros_like(left_site))
    keep_right = (
        charge_next[:, None, None, None]
        + link_next[None, :, None, None]
        - link_next[None, None, :, None]
        == fresh_next[None, None, None, :]
    )
    masked_right = jnp.where(keep_right, right_site, jnp.zeros_like(right_site))
    first = jnp.einsum(
        "xalm,auvb->xlmuvb", masked_left, masked_mps, preferred_element_type=jnp.float32
    ).astype(jnp.bfloat16)
    second = jnp.einsum(
        "xlmuvb,uldrp->xmvbdrp", first, masked_ket, preferred_element_type=jnp.float32
    ).astype(jnp.bfloat16)
    third = jnp.einsum(
        "xmvbdrp,vmesp->xbdres", second, masked_ket, preferred_element_type=jnp.float32
    ).astype(jnp.bfloat16)
    return jnp.einsum("xbdres,brsy->xdey", third, masked_right, preferred_element_type=jnp.float32)


def local(mps, ket, left_proj, right_proj, bond_charge, new_charge, link_charge, vert_charge):
    sites_here = mps.shape[0]
    half = left_proj.shape[1]
    full_mps = lax.all_gather(mps, "sec", axis=1, tiled=True)
    chi_full = full_mps.shape[1]
    legs = full_mps.shape[2]
    received = from_behind((bond_charge, new_charge, link_charge), COL, -1)
    bond_next = jnp.concatenate([bond_charge[1:], received[0]], axis=0)
    fresh_next = jnp.concatenate([new_charge[1:], received[1]], axis=0)
    link_next = jnp.concatenate([link_charge[1:], received[2]], axis=0)
    arrived = from_behind(right_proj, COL, -1)
    partial_next = jnp.concatenate([right_proj[1:], arrived], axis=0)
    right_next = gather_directly(partial_next, "sec", 4)
    offset = lax.axis_index("sec") * half
    fresh_half = lax.dynamic_slice_in_dim(new_charge[0], offset, half, 0)
    images = [
        absorb(
            full_mps[0],
            ket[0],
            left_proj[0],
            right_next[0],
            bond_charge[0],
            bond_next[0],
            fresh_half,
            fresh_next[0],
            link_charge[0],
            link_next[0],
            vert_charge[0],
        )
    ]
    image = jnp.stack(images, axis=0)
    partial_value = jnp.sum(image * image, axis=(1, 2, 3, 4))
    count = chi_full * legs * legs * chi_full
    columns = lax.axis_size(COL)
    squares = gathered_total(partial_value, "sec")
    meansq = squares / count
    logs = 0.5 * jnp.log(meansq + 1e-06)
    total = one_axis_at_a_time(jnp.sum(logs), COL)
    log_norm = total / (sites_here * columns)
    scale = lax.rsqrt(meansq + 1e-06)
    new_mps = (image * scale[:, None, None, None, None]).astype(jnp.bfloat16)
    return (new_mps, log_norm)


def solution(mesh):
    torus = Mesh(
        mesh.devices.reshape(4, 8, 4, mesh.shape["sec"]), ("col_0", "col_1", "col_2", "sec")
    )
    in_specs = (
        P(COL, "sec", None, None, None),
        P(COL, None, None, None, None, None),
        P(COL, "sec", None, None, None),
        P(COL, None, None, None, "sec"),
        P(COL, None),
        P(COL, None),
        P(COL, None),
        P(COL, None, None),
    )
    out_specs = (P(COL, "sec", None, None, None), P())
    return jax.shard_map(local, mesh=torus, in_specs=in_specs, out_specs=out_specs, check_vma=False)
```

profile of v0, /device:TPU:32, one launch (start us, length us, event | category | flops | bytes accessed | tf_op | source)
XLA Modules:
  0.0 162.3 jit_solution(1129275034538465947)
XLA Ops:
  0.6 2.6 %collective-permute-start = (s32[1,96]{1,0:T(1,128)}, s32[1,96]{1,0:T(1,128)S(1)}, u32[]{:S(2)}, u32[]{:S(2)}) collective-permute-start(s32[1,96]{1,0:T(1,128)} %param.12), channel_id=1, source_target_pairs={{0,254},{2,0},{4,2},{6,4},{8,6},{10,8},{12,10},{14,12},{16,14},{18... | collective-permute-start | bytes 1160 | tf_op jit(solution)/shard_map/ppermute | solution.py:13
  3.3 0.7 collective-permute-start.1
  4.5 2.2 %collective-permute-start.2 = (s32[1,96]{1,0:T(1,128)}, s32[1,96]{1,0:T(1,128)S(1)}, u32[]{:S(2)}, u32[]{:S(2)}) collective-permute-start(s32[1,96]{1,0:T(1,128)} %param.13), channel_id=1, source_target_pairs={{0,254},{2,0},{4,2},{6,4},{8,6},{10,8},{12,10},{14,12},{16,14},{18... | collective-permute-start | bytes 1160 | tf_op jit(solution)/shard_map/ppermute | solution.py:13
  6.6 0.8 slice_bitcast_fusion
  7.4 0.7 broadcast_add_fusion.2
  8.1 0.7 broadcast_add_fusion.4
  8.9 0.7 dynamic-slice_bitcast_fusion
  9.6 0.7 broadcast_subtract_fusion.2
  10.4 4.4 %all_gather.9 = bf16[1,96,6,6,96]{4,1,3,2,0:T(8,128)(2,1)} all-gather(bf16[1,48,6,6,96]{4,1,3,2,0:T(8,128)(2,1)} %param.8), channel_id=1, replica_groups=mesh['col_0'=4,'col_1'=8,'col_2'=4,'sec'=2] {'sec'}, dimensions={1}, use_global_device_ids=true | all-gather | bytes 995328 | tf_op jit(solution)/shard_map/all_gather | solution.py:97
  14.7 1.3 dynamic-slice.1
  16.1 1.1 fusion.29
  17.2 5.8 %convert_bitcast_fusion = bf16[48,6,6,6,6,96,1,1]{5,0,4,3,2,1,7,6:T(8,128)(2,1)S(1)} fusion(bf16[1,96,6,6,96]{4,1,3,2,0:T(8,128)(2,1)} %all_gather.9, s32[96]{0:T(128)S(1)} %bitcast.67, s32[96,6,6]{0,2,1:T(8,128)S(1)} %broadcast_subtract_fusion.1, bf16[1,48,96,6,6]{2,1,4,3,0:T(8,128)(2,1)} %param.10, s32[96,6,6]{0,2,1:T(8,128)S(1)} %broadcast_subtract_fusion.2, ...), kind=kOutput, calls=%fused_computation.8 | convolution fusion | flops 1153585152 | bytes 12967488 | tf_op jit(solution)/shard_map/xalm,auvb->xlmuvb/dot_general | solution.py:82
  23.1 28.1 %fusion = bf16[48,6,6,96,6,6,2,1]{3,5,6,4,2,1,0,7:T(8,128)(2,1)} fusion(bf16[48,6,6,6,6,96,1,1]{5,0,4,3,2,1,7,6:T(8,128)(2,1)S(1)} %convert_bitcast_fusion, bf16[6,6,6,6,2,1,1,1]{3,4,2,1,0,7,6,5:T(2,128)(2,1)S(1)} %fusion.29), kind=kOutput, calls=%fused_computation.1 | convolution fusion | flops 871907328 | bytes 35836992 | tf_op jit(solution)/shard_map/xlmuvb,uldrp->xmvbdrp/dot_general | solution.py:85
  51.1 38.6 %bitcast_convert_fusion.1 = bf16[48,96,6,6,6,6]{1,5,4,3,2,0:T(8,128)(2,1)} fusion(bf16[48,6,6,96,6,6,2,1]{3,5,6,4,2,1,0,7:T(8,128)(2,1)} %fusion, bf16[6,6,6,6,2,1,1,1]{3,4,2,1,0,7,6,5:T(2,128)(2,1)S(1)} %fusion.29), kind=kOutput, calls=%fused_computation.2 | convolution fusion | flops 865935360 | bytes 35836992 | tf_op jit(solution)/shard_map/xmvbdrp,vmesp->xbdres/dot_general | solution.py:88
  89.8 1.1 broadcast_in_dim.20
  91.0 4.5 %all_to_all.5 = bf16[2,1,96,6,6,48]{2,5,4,3,1,0:T(8,128)(2,1)S(1)} all-to-all(bf16[2,1,96,6,6,48]{2,5,4,3,1,0:T(8,128)(2,1)S(1)} %broadcast_in_dim.20), channel_id=1, replica_groups=mesh['col_0'=4,'col_1'=8,'col_2'=4,'sec'=2] {'sec'}, dimensions={0} | all-to-all | bytes 1327104 | tf_op jit(solution)/shard_map/all_to_all | solution.py:24
  95.6 17.4 %multiply_reduce_fusion = (f32[]{:T(128)}, f32[48,6,6,96]{3,0,2,1:T(8,128)S(1)}) fusion(bf16[96,6,6,96]{0,3,2,1:T(8,128)(2,1)S(1)} %bitcast.60, s32[96,6,6]{0,2,1:T(8,128)S(1)} %broadcast_subtract_fusion, s32[96]{0:T(128)S(1)} %bitcast.70, bf16[48,96,6,6,6,6]{1,5,4,3,2,0:T(8,128)(2,1)} %bitcast_convert_fusion.1), kind=kOutput, calls=%fused_computation.15 | convolution fusion | flops 1147613184 | bytes 13285252 | tf_op jit(solution)/shard_map/xbdres,brsy->xdey/dot_general | solution.py:91
  112.9 1.4 dynamic-update-slice
  114.3 2.4 %all-reduce = f32[2]{0:T(128)S(1)} all-reduce(f32[2]{0:T(128)S(1)} %dynamic-update-slice), channel_id=1, replica_groups=mesh['col_0'=4,'col_1'=8,'col_2'=4,'sec'=2] {'sec'}, use_global_device_ids=true, to_apply=%add | all-reduce | flops 2 | bytes 16
  116.8 0.6 reduce.3
  118.1 9.3 %psum.21 = f32[]{:T(128)} all-reduce(f32[]{:T(128)S(6)} %mul.24), channel_id=1, replica_groups=mesh['col_0'=4,'col_1'=8,'col_2'=4,'sec'=2] {'col_0'}, use_global_device_ids=true, to_apply=%region_2.3 | all-reduce | flops 1 | bytes 8 | tf_op jit(solution)/shard_map/psum | solution.py:37
  127.4 20.9 %psum.22 = f32[]{:T(128)} all-reduce(f32[]{:T(128)} %psum.21), channel_id=1, replica_groups=mesh['col_0'=4,'col_1'=8,'col_2'=4,'sec'=2] {'col_1'}, use_global_device_ids=true, to_apply=%region_3.4 | all-reduce | flops 1 | bytes 8 | tf_op jit(solution)/shard_map/psum | solution.py:37
  148.3 11.4 %psum.23 = f32[]{:T(128)} all-reduce(f32[]{:T(128)} %psum.22), channel_id=1, replica_groups=mesh['col_0'=4,'col_1'=8,'col_2'=4,'sec'=2] {'col_2'}, use_global_device_ids=true, to_apply=%region_4.5 | all-reduce | flops 1 | bytes 8 | tf_op jit(solution)/shard_map/psum | solution.py:37
  159.7 0.8 fusion.21
  (12 shorter events, 0.8 us)
Async XLA Ops:
  0.6 16.6 %collective-permute-start = (s32[1,96]{1,0:T(1,128)}, s32[1,96]{1,0:T(1,128)S(1)}, u32[]{:S(2)}, u32[]{:S(2)}) collective-permute-start(s32[1,96]{1,0:T(1,128)} %param.12), channel_id=1, source_target_pairs={{0,254},{2,0},{4,2},{6,4},{8,6},{10,8},{12,10},{14,12},{16,14},{18... | collective-permute-start | bytes 1160 | tf_op jit(solution)/shard_map/ppermute | solution.py:13
  3.3 12.7 %collective-permute-start.1 = (s32[1,6]{1,0:T(1,128)}, s32[1,6]{1,0:T(1,128)S(1)}, u32[]{:S(2)}, u32[]{:S(2)}) collective-permute-start(s32[1,6]{1,0:T(1,128)} %param.14), channel_id=1, source_target_pairs={{0,254},{2,0},{4,2},{6,4},{8,6},{10,8},{12,10},{14,12},{16,14},{18... | collective-permute-start | bytes 80 | tf_op jit(solution)/shard_map/ppermute | solution.py:13
  4.0 85.8 %collective-permute-start.3 = (bf16[1,96,6,6,48]{1,4,3,2,0:T(8,128)(2,1)}, bf16[1,96,6,6,48]{1,4,3,2,0:T(8,128)(2,1)}, u32[]{:S(2)}, u32[]{:S(2)}) collective-permute-start(bf16[1,96,6,6,48]{1,4,3,2,0:T(8,128)(2,1)} %param.11), channel_id=1, source_target_pairs={{0,254},{2,0},{4,2},{6,4},{8,6},{10,8},{12,10},{14,12},{16,14},{18... | collective-permute-start | bytes 995336 | tf_op jit(solution)/shard_map/ppermute | solution.py:13
  4.5 91.1 %collective-permute-start.2 = (s32[1,96]{1,0:T(1,128)}, s32[1,96]{1,0:T(1,128)S(1)}, u32[]{:S(2)}, u32[]{:S(2)}) collective-permute-start(s32[1,96]{1,0:T(1,128)} %param.13), channel_id=1, source_target_pairs={{0,254},{2,0},{4,2},{6,4},{8,6},{10,8},{12,10},{14,12},{16,14},{18... | collective-permute-start | bytes 1160 | tf_op jit(solution)/shard_map/ppermute | solution.py:13
where the time goes:
time: 163 us; the launch traced here: 162 us
  matrix products  89.8 us (55%)
  blocking collectives  52.9 us (32%)
  starting transfers between devices  5.99 us (4%)
  local copies, waits for them, and re-layouts  5.34 us (3%)
  other arithmetic  5.05 us (3%)
  between operations  3.21 us (2%)
    psum x3, blocking collectives, one_axis_at_a_time(): return functools.reduce(lax.psum, axes, x)  41.6 us
    dot_general x1, matrix products, absorb(): jnp.einsum('xmvbdrp,vmesp->xbdres', second, masked_ket, preferred_element...  38.6 us
    dot_general x1, matrix products, absorb(): jnp.einsum('xlmuvb,uldrp->xmvbdrp', first, masked_ket, preferred_element_...  28.1 us
    dot_general x1, matrix products, absorb(): jnp.einsum('xbdres,brsy->xdey', third, masked_right, preferred_element_ty...  17.4 us
    ppermute x4, starting transfers between devices, from_behind(): return lax.ppermute(x, axis, [(i, (i + by) % count) for i in range(count)])  5.99 us
    dot_general x1, matrix products, absorb(): jnp.einsum('xalm,auvb->xlmuvb', masked_left, masked_mps, preferred_elemen...  5.81 us
    all_to_all x1, blocking collectives, copy_for_each(): lax.all_to_all(jnp.broadcast_to(x[None], (count, *x.shape)), axis, 0, 0,...  4.52 us
    all_gather x1, blocking collectives, local(): full_mps = lax.all_gather(mps, 'sec', axis=1, tiled=True)  4.38 us
  transfers between devices with their start and end apart: 4, of which 0 were waited for; matrix products, arithmetic and copies ran while one was open for 49% of the time, Pallas kernels for 0%

commit v1 on v0

--- a/solution.py
+++ b/solution.py
@@ -4,8 +4,22 @@
 from jax import lax
 from jax.sharding import Mesh
 from jax.sharding import PartitionSpec as P
+from jax.lax import all_to_all, axis_size
 
 COL = ("col_0", "col_1", "col_2")
+
+
+def register_the_lines(tile_in, dev_axis, array_axis):
+    xs_all = []
+    for _ in range(axis_size(dev_axis)):
+        xs_all.append(tile_in)
+    extra = jnp.concatenate(
+        all_to_all(jnp.stack(xs_all), dev_axis, split_axis=0, concat_axis=0), axis=array_axis
+    )
+    return extra
+
+
+render_the_side = functools.partial(register_the_lines, dev_axis="sec", array_axis=1)
 
 
 def from_behind(x, axis, by):
@@ -94,7 +108,7 @@
 def local(mps, ket, left_proj, right_proj, bond_charge, new_charge, link_charge, vert_charge):
     sites_here = mps.shape[0]
     half = left_proj.shape[1]
-    full_mps = lax.all_gather(mps, "sec", axis=1, tiled=True)
+    full_mps = render_the_side(mps)
     chi_full = full_mps.shape[1]
     legs = full_mps.shape[2]
     received = from_behind((bond_charge, new_charge, link_charge), COL, -1)

time: 163 us -> 168 us (1.031)
  blocking collectives: 52.9 us -> 48.4 us
  other arithmetic: 5.05 us -> 9.43 us
  starting transfers between devices: 5.99 us -> 9.61 us
    all_gather x1 -> x0, blocking collectives: 4.38 us -> none  [local(): full_mps = lax.all_gather(mps, 'sec', axis=1, tiled=True)]
    all_to_all x0 -> x1, starting transfers between devices: none -> 3.55 us  [register_the_lines(): all_to_all(jnp.stack(xs_all), dev_axis, split_axis=0, concat_axis=0)]
    dot_general x1, matrix products: 5.81 us -> 8.83 us  [absorb(): jnp.einsum('xalm,auvb->xlmuvb', masked_left, masked_mps, preferred_elemen...]
    another operation x0 -> x1, other arithmetic: none -> 2.27 us  [register_the_lines(): jnp.stack(xs_all)]
  transfers between devices with their start and end apart: 4 -> 5, of which waited for: 0 -> 0; matrix products, arithmetic and copies ran while one was open for 49% -> 51% of each run, Pallas kernels for 0% -> 0%
where the time goes in v1:
time: 168 us; the launch traced here: 167 us
  matrix products  91.3 us (54%)
  blocking collectives  48.4 us (29%)
  starting transfers between devices  9.61 us (6%)
  other arithmetic  9.43 us (6%)
  local copies, waits for them, and re-layouts  4.96 us (3%)
  between operations  3.23 us (2%)
    psum x3, blocking collectives, one_axis_at_a_time(): return functools.reduce(lax.psum, axes, x)  41.5 us
    dot_general x1, matrix products, absorb(): jnp.einsum('xmvbdrp,vmesp->xbdres', second, masked_ket, preferred_element...  38.6 us
    dot_general x1, matrix products, absorb(): jnp.einsum('xlmuvb,uldrp->xmvbdrp', first, masked_ket, preferred_element_...  26.5 us
    dot_general x1, matrix products, absorb(): jnp.einsum('xbdres,brsy->xdey', third, masked_right, preferred_element_ty...  17.4 us
    dot_general x1, matrix products, absorb(): jnp.einsum('xalm,auvb->xlmuvb', masked_left, masked_mps, preferred_elemen...  8.83 us
    ppermute x4, starting transfers between devices, from_behind(): return lax.ppermute(x, axis, [(i, (i + by) % count) for i in range(count)])  6.06 us
    all_to_all x1, blocking collectives, copy_for_each(): lax.all_to_all(jnp.broadcast_to(x[None], (count, *x.shape)), axis, 0, 0,...  4.43 us
    all_to_all x1, starting transfers between devices, register_the_lines(): all_to_all(jnp.stack(xs_all), dev_axis, split_axis=0, concat_axis=0)  3.55 us
  transfers between devices with their start and end apart: 5, of which 0 were waited for; matrix products, arithmetic and copies ran while one was open for 51% of the time, Pallas kernels for 0%

profile of v1, /device:TPU:32, one launch (start us, length us, event | category | flops | bytes accessed | tf_op | source)
XLA Modules:
  0.0 166.9 jit_solution(8796686511866597362)
XLA Ops:
  0.6 2.6 %collective-permute-start = (s32[1,96]{1,0:T(1,128)}, s32[1,96]{1,0:T(1,128)S(1)}, u32[]{:S(2)}, u32[]{:S(2)}) collective-permute-start(s32[1,96]{1,0:T(1,128)} %param.12), channel_id=1, source_target_pairs={{0,254},{2,0},{4,2},{6,4},{8,6},{10,8},{12,10},{14,12},{16,14},{18... | collective-permute-start | bytes 1160 | tf_op jit(solution)/shard_map/ppermute | solution.py:27
  3.3 2.3 %pad_maximum_fusion = bf16[2,1,48,6,6,96]{5,2,4,3,1,0:T(8,128)(2,1)} fusion(bf16[1,1,48,6,6,96]{5,2,4,3,1,0:T(8,128)(2,1)} %bitcast.62), kind=kLoop, calls=%fused_computation.13 | loop fusion | flops 331776 | bytes 995328 | tf_op jit(solution)/shard_map/stack | solution.py:17
  5.5 3.6 %all-to-all-start = ((bf16[2,1,48,6,6,96]{5,2,4,3,1,0:T(8,128)(2,1)}), bf16[2,1,48,6,6,96]{5,2,4,3,1,0:T(8,128)(2,1)S(1)}, u32[]{:S(2)}, u32[]{:S(2)}) async-start(bf16[2,1,48,6,6,96]{5,2,4,3,1,0:T(8,128)(2,1)} %pad_maximum_fusion), calls=%async_computation | async-start | bytes 1769472 | tf_op jit(solution)/shard_map/all_to_all | solution.py:17
  9.1 0.8 collective-permute-start.1
  10.4 2.2 %collective-permute-start.2 = (s32[1,96]{1,0:T(1,128)}, s32[1,96]{1,0:T(1,128)S(1)}, u32[]{:S(2)}, u32[]{:S(2)}) collective-permute-start(s32[1,96]{1,0:T(1,128)} %param.13), channel_id=1, source_target_pairs={{0,254},{2,0},{4,2},{6,4},{8,6},{10,8},{12,10},{14,12},{16,14},{18... | collective-permute-start | bytes 1160 | tf_op jit(solution)/shard_map/ppermute | solution.py:27
  12.5 0.8 dynamic-slice_bitcast_fusion
  13.3 0.8 slice_bitcast_fusion
  14.6 1.3 reduce.8
  16.1 0.7 broadcast_add_fusion.3
  16.8 0.7 broadcast_add_fusion.4
  17.6 0.7 broadcast_subtract_fusion.2
  18.3 1.3 dynamic-slice.1
  19.7 1.1 fusion.24
  21.5 8.8 %convert_bitcast_fusion = bf16[48,6,6,6,6,96,1,1]{5,0,4,3,2,1,7,6:T(8,128)(2,1)} fusion(bf16[96,6,6,96,1,1]{3,0,2,1,5,4:T(8,128)(2,1)S(1)} %bitcast.60, bf16[1,48,96,6,6]{2,1,4,3,0:T(8,128)(2,1)} %param.10, s32[96,6,6]{0,2,1:T(8,128)S(1)} %broadcast_subtract_fusion.2, s32[48]{0:T(128)S(1)} %dynamic-slice_bitcast_fusion), kind=kOutput, calls=%fused_computation.8 | convolution fusion | flops 1152921600 | bytes 12953280 | tf_op jit(solution)/shard_map/xalm,auvb->xlmuvb/dot_general | solution.py:96
  30.4 26.5 %fusion = bf16[48,6,6,96,6,6,2,1]{3,5,6,4,2,1,0,7:T(8,128)(2,1)} fusion(bf16[48,6,6,6,6,96,1,1]{5,0,4,3,2,1,7,6:T(8,128)(2,1)} %convert_bitcast_fusion, bf16[6,6,6,6,2,1,1,1]{3,4,2,1,0,7,6,5:T(2,128)(2,1)S(1)} %fusion.24), kind=kOutput, calls=%fused_computation.1 | convolution fusion | flops 871907328 | bytes 35836992 | tf_op jit(solution)/shard_map/xlmuvb,uldrp->xmvbdrp/dot_general | solution.py:99
  56.9 38.6 %bitcast_convert_fusion.1 = bf16[48,96,6,6,6,6]{1,5,4,3,2,0:T(8,128)(2,1)} fusion(bf16[48,6,6,96,6,6,2,1]{3,5,6,4,2,1,0,7:T(8,128)(2,1)} %fusion, bf16[6,6,6,6,2,1,1,1]{3,4,2,1,0,7,6,5:T(2,128)(2,1)S(1)} %fusion.24), kind=kOutput, calls=%fused_computation.2 | convolution fusion | flops 865935360 | bytes 35836992 | tf_op jit(solution)/shard_map/xmvbdrp,vmesp->xbdres/dot_general | solution.py:102
  95.7 4.4 %all_to_all.10 = bf16[2,1,96,6,6,48]{2,5,4,3,1,0:T(8,128)(2,1)S(1)} all-to-all(bf16[2,1,96,6,6,48]{2,5,4,3,1,0:T(8,128)(2,1)S(1)} %broadcast_in_dim.20), channel_id=1, replica_groups=mesh['col_0'=4,'col_1'=8,'col_2'=4,'sec'=2] {'sec'}, dimensions={0} | all-to-all | bytes 1327104 | tf_op jit(solution)/shard_map/all_to_all | solution.py:38
  100.2 17.4 %multiply_reduce_fusion = (f32[]{:T(128)}, f32[48,6,6,96]{3,0,2,1:T(8,128)S(1)}) fusion(bf16[96,6,6,96]{0,3,2,1:T(8,128)(2,1)S(1)} %bitcast.61, s32[96,6,6]{0,2,1:T(8,128)S(1)} %broadcast_subtract_fusion.1, s32[96]{0:T(128)S(1)} %bitcast.73, bf16[48,96,6,6,6,6]{1,5,4,3,2,0:T(8,128)(2,1)} %bitcast_convert_fusion.1), kind=kOutput, calls=%fused_computation.15 | convolution fusion | flops 1147613184 | bytes 13285252 | tf_op jit(solution)/shard_map/xbdres,brsy->xdey/dot_general | solution.py:105
  117.6 1.4 dynamic-update-slice
  119.0 2.4 %all-reduce = f32[2]{0:T(128)S(1)} all-reduce(f32[2]{0:T(128)S(1)} %dynamic-update-slice), channel_id=1, replica_groups=mesh['col_0'=4,'col_1'=8,'col_2'=4,'sec'=2] {'sec'}, use_global_device_ids=true, to_apply=%add | all-reduce | flops 2 | bytes 16
  122.7 9.3 %psum.21 = f32[]{:T(128)} all-reduce(f32[]{:T(128)S(6)} %mul.24), channel_id=1, replica_groups=mesh['col_0'=4,'col_1'=8,'col_2'=4,'sec'=2] {'col_0'}, use_global_device_ids=true, to_apply=%region_2.3 | all-reduce | flops 1 | bytes 8 | tf_op jit(solution)/shard_map/psum | solution.py:51
  132.0 20.9 %psum.22 = f32[]{:T(128)} all-reduce(f32[]{:T(128)} %psum.21), channel_id=1, replica_groups=mesh['col_0'=4,'col_1'=8,'col_2'=4,'sec'=2] {'col_1'}, use_global_device_ids=true, to_apply=%region_3.4 | all-reduce | flops 1 | bytes 8 | tf_op jit(solution)/shard_map/psum | solution.py:51
  152.9 11.4 %psum.23 = f32[]{:T(128)} all-reduce(f32[]{:T(128)} %psum.22), channel_id=1, replica_groups=mesh['col_0'=4,'col_1'=8,'col_2'=4,'sec'=2] {'col_2'}, use_global_device_ids=true, to_apply=%region_4.5 | all-reduce | flops 1 | bytes 8 | tf_op jit(solution)/shard_map/psum | solution.py:51
  164.3 0.8 fusion.17
  (19 shorter events, 2.9 us)
Async XLA Ops:
  0.6 20.2 %collective-permute-start = (s32[1,96]{1,0:T(1,128)}, s32[1,96]{1,0:T(1,128)S(1)}, u32[]{:S(2)}, u32[]{:S(2)}) collective-permute-start(s32[1,96]{1,0:T(1,128)} %param.12), channel_id=1, source_target_pairs={{0,254},{2,0},{4,2},{6,4},{8,6},{10,8},{12,10},{14,12},{16,14},{18... | collective-permute-start | bytes 1160 | tf_op jit(solution)/shard_map/ppermute | solution.py:27
  5.5 15.3 %all-to-all-start = ((bf16[2,1,48,6,6,96]{5,2,4,3,1,0:T(8,128)(2,1)}), bf16[2,1,48,6,6,96]{5,2,4,3,1,0:T(8,128)(2,1)S(1)}, u32[]{:S(2)}, u32[]{:S(2)}) async-start(bf16[2,1,48,6,6,96]{5,2,4,3,1,0:T(8,128)(2,1)} %pad_maximum_fusion), calls=%async_computation | async-start | bytes 1769472 | tf_op jit(solution)/shard_map/all_to_all | solution.py:17
  9.1 10.5 %collective-permute-start.1 = (s32[1,6]{1,0:T(1,128)}, s32[1,6]{1,0:T(1,128)S(1)}, u32[]{:S(2)}, u32[]{:S(2)}) collective-permute-start(s32[1,6]{1,0:T(1,128)} %param.14), channel_id=1, source_target_pairs={{0,254},{2,0},{4,2},{6,4},{8,6},{10,8},{12,10},{14,12},{16,14},{18... | collective-permute-start | bytes 80 | tf_op jit(solution)/shard_map/ppermute | solution.py:27
  9.9 85.7 %collective-permute-start.3 = (bf16[1,96,6,6,48]{1,4,3,2,0:T(8,128)(2,1)}, bf16[1,96,6,6,48]{1,4,3,2,0:T(8,128)(2,1)S(1)}, u32[]{:S(2)}, u32[]{:S(2)}) collective-permute-start(bf16[1,96,6,6,48]{1,4,3,2,0:T(8,128)(2,1)} %param.11), channel_id=1, source_target_pairs={{0,254},{2,0},{4,2},{6,4},{8,6},{10,8},{12,10},{14,12},{16,14},{18... | collective-permute-start | bytes 995336 | tf_op jit(solution)/shard_map/ppermute | solution.py:27
  10.4 89.8 %collective-permute-start.2 = (s32[1,96]{1,0:T(1,128)}, s32[1,96]{1,0:T(1,128)S(1)}, u32[]{:S(2)}, u32[]{:S(2)}) collective-permute-start(s32[1,96]{1,0:T(1,128)} %param.13), channel_id=1, source_target_pairs={{0,254},{2,0},{4,2},{6,4},{8,6},{10,8},{12,10},{14,12},{16,14},{18... | collective-permute-start | bytes 1160 | tf_op jit(solution)/shard_map/ppermute | solution.py:27
